TPU v7x, 32 devices: a whole 2x2x4 slice. The times are simulated.
32 devices in a mesh: dev: 32 (over z, y, x, core).
Axes of the slice: x: 2, y: 2, z: 4, core: 2. Of those that a mesh axis runs over, the one named last changes fastest.
Arguments:
- image_feats: bfloat16 [384, 1152], P('dev'), may hold values from -0.1875 to 0.1875
- text_feats: bfloat16 [384, 1152], P('dev'), may hold values from -0.1875 to 0.1875
- image_head: bfloat16 [1152, 640], replicated, may hold values from -0.1875 to 0.1875
- text_head: bfloat16 [1152, 640], replicated, may hold values from -0.1875 to 0.1875
- log_scale: float32 [], replicated, may hold values from 1.6 to 2.3
- logit_bias: float32 [], replicated, may hold values from -8 to -4
- image_group: int32 [384], P('dev'), may hold values from 0 to 191
- text_group: int32 [384], P('dev'), may hold values from 0 to 191
Outputs:
- loss: float32 [], replicated
- grad_images: bfloat16 [384, 1152], P('dev')
- grad_texts: bfloat16 [384, 1152], P('dev')
- grad_scale: float32 [], replicated
- grad_bias: float32 [], replicated
All inputs are finite; a program needn't handle non-finite values.
Results may differ from a plain program's by a relative error of at most 0.0063.
Values may be sent and summed in bfloat16 or wider, within the bound.
No kernel may reach another device: no remote copies, remote signals or barrier semaphores. Data moves between devices by JAX's collectives and lax.ppermute only.
A program may use at most 128 MiB of HBM per device.

v0:
```python
import functools

import jax
import jax.numpy as jnp
from jax import lax
from jax.experimental import pallas as pl
from jax.experimental.pallas import tpu as pltpu
from jax.sharding import PartitionSpec as P


epsilon = 1e-06
LANES = 128
TILE = 8
BITS = 32
LOGIT_BUDGET = 4 << 20
SIDE_FLOPS = 1 << 26


def normalize(projected):
    length = jnp.sqrt(jnp.sum(projected * projected, axis=1, keepdims=True) + epsilon)
    return (projected / length, length)


def contract_last(a, b):
    return lax.dot_general(a, b, (((1,), (1,)), ((), ())), preferred_element_type=jnp.float32)


def backward_rows(grad_unit, unit_vec, length, weights):
    inner = jnp.sum(unit_vec * grad_unit, axis=1, keepdims=True)
    grad_proj = ((grad_unit - unit_vec * inner) / length).astype(jnp.bfloat16)
    return contract_last(grad_proj, weights).astype(jnp.bfloat16)


def on_device_large(
    image_feats, text_feats, image_head, text_head, log_scale, logit_bias, image_group, text_group
):
    img_unit, img_length = normalize(
        jnp.dot(image_feats, image_head, preferred_element_type=jnp.float32)
    )
    txt_unit, txt_length = normalize(
        jnp.dot(text_feats, text_head, preferred_element_type=jnp.float32)
    )
    img_emb = img_unit.astype(jnp.bfloat16)
    txt_emb = txt_unit.astype(jnp.bfloat16)
    logit_scale = jnp.exp(log_scale)
    pairs = image_feats.shape[0] * lax.axis_size("dev")
    emb_piece = lax.all_gather(jnp.stack([img_emb, txt_emb]), "dev", axis=1, tiled=True)
    id_piece = lax.all_gather(jnp.stack([image_group, text_group]), "dev", axis=1, tiled=True)

    def side(emb, others, group, other_group):
        cosine = contract_last(emb, others)
        label = jnp.where(group[:, None] == other_group[None, :], 1.0, -1.0).astype(jnp.float32)
        margin = label * (logit_scale * cosine + logit_bias)
        slopes = -label * jax.nn.sigmoid(-margin)
        grad = logit_scale * jnp.dot(
            slopes.astype(jnp.bfloat16), others, preferred_element_type=jnp.float32
        )
        return cosine, margin, slopes, grad

    cosine, margin, slopes, grad_img = side(img_emb, emb_piece[1], image_group, id_piece[1])
    local_sums = jnp.stack(
        [jnp.sum(jax.nn.softplus(-margin)), jnp.sum(slopes * cosine), jnp.sum(slopes)]
    )
    grad_txt = side(txt_emb, emb_piece[0], text_group, id_piece[0])[3]
    totals = lax.psum(local_sums, "dev")
    return (
        totals[0] / pairs,
        backward_rows(grad_img, img_unit, img_length, image_head),
        backward_rows(grad_txt, txt_unit, txt_length, text_head),
        logit_scale * totals[1] / pairs,
        totals[2] / pairs,
    )


def project_kernel(
    image_ids, text_ids, image_feats, text_feats, image_head, text_head,
    payload, img_kept, txt_kept,
    image_kept, text_kept, frame, image_rows, text_rows,
    image_marks, text_marks, head_sems, sems,
):
    rows, width = image_feats.shape[0], image_head.shape[1]
    depth, chunks = image_head.shape[0], head_sems.shape[1]
    step = depth // chunks
    odd = lax.rem(lax.axis_index("dev"), 2) == 1
    small = [
        pltpu.make_async_copy(source, target, sems.at[i])
        for i, (source, target) in enumerate(
            (
                (image_feats, image_rows),
                (text_feats, text_rows),
                (image_ids, image_marks),
                (text_ids, text_marks),
            )
        )
    ]
    large = [
        [
            pltpu.make_async_copy(
                head.at[pl.ds(i * step, step)], kept.at[pl.ds(i * step, step)], head_sems.at[side, i]
            )
            for i in range(chunks)
        ]
        for side, (head, kept) in enumerate(((image_head, image_kept), (text_head, text_kept)))
    ]
    small[0].start()
    for copy in large[0]:
        copy.start()
    for copy in small[1:]:
        copy.start()
    for copy in large[1]:
        copy.start()

    units = []
    sides = (
        (image_rows, image_kept, img_kept),
        (text_rows, text_kept, txt_kept),
    )
    for side, (feats, kept, out) in enumerate(sides):
        small[side].wait()
        projected = jnp.zeros((rows, width), jnp.float32)
        for i, copy in enumerate(large[side]):
            copy.wait()
            part = slice(i * step, (i + 1) * step)
            projected += jnp.dot(feats[:, part], kept[part], preferred_element_type=jnp.float32)
        unit, length = normalize(projected)
        out[:, :width] = unit
        out[:, width:] = jnp.broadcast_to(length, (rows, LANES))
        units.append(unit)
    frame[:rows] = jnp.where(odd, units[1], units[0])
    frame[rows:] = jnp.where(odd, units[0], units[1])
    groups = 2 * rows // TILE
    for block in range(width // LANES):
        columns = slice(block * LANES, (block + 1) * LANES)
        for group in range(groups):
            part = frame[group * TILE : (group + 1) * TILE, columns]
            payload[block * groups + group] = part.astype(jnp.bfloat16)

    for copy in small[2:]:
        copy.wait()
    position = lax.broadcasted_iota(jnp.int32, (TILE, LANES), 0)
    lane = lax.broadcasted_iota(jnp.int32, (TILE, LANES), 1)
    position += TILE * (lane // BITS)
    ids = jnp.zeros((TILE, LANES), jnp.int32)
    for row in range(rows):
        image_id, text_id = image_marks[row], text_marks[row]
        ids = jnp.where(position == row, jnp.where(odd, text_id, image_id), ids)
        ids = jnp.where(position == rows + row, jnp.where(odd, image_id, text_id), ids)
    bits = lax.shift_right_logical(ids, lane & (BITS - 1)) & 1
    payload[payload.shape[0] - 1] = jnp.where(bits == 1, 1.0, -1.0).astype(jnp.bfloat16)


def hop_orders(devices):
    bits = [1 << level for level in reversed(range(1, devices.bit_length() - 1))]
    first, rest = bits[:1], bits[1:]
    return first + rest, first + rest[1:] + rest[:1]


def parity(number, bits):
    return sum((number >> level) & 1 for level in range(bits)) % 2


def slot_of(apart, order):
    hops = [int(apart & bit != 0) for bit in order]
    return hops[-1] + 2 * hops[-2] + 4 * sum(hop << level for level, hop in enumerate(hops[:-2]))


def frame_of(ref, slot, block, groups, lane):
    if (block + 1) * groups < ref.shape[1]:
        tiles = ref[slot, block * groups : (block + 1) * groups].astype(jnp.float32)
        return tiles.reshape(groups * TILE, LANES)
    packed = ref[slot, ref.shape[1] - 1].astype(jnp.float32)
    turned = [packed] + [
        pltpu.roll(packed, LANES - group * BITS, axis=1) for group in range(1, groups)
    ]
    return jnp.where(lane < BITS, jnp.concatenate(turned, axis=0), 0.0)


def pair_terms(cosine, matches, scale, bias):
    label = jnp.where(matches > BITS - 1.0, 1.0, -1.0)
    negative = -label * (scale * cosine + bias)
    decay = jnp.exp(-jnp.abs(negative))
    inverse = 1.0 / (1.0 + decay)
    slopes = -label * jnp.where(negative >= 0.0, inverse, decay * inverse)
    return negative, decay, slopes


def loss_kernel(chips, pairs, orders, *refs):
    mine_pieces, other_pieces = refs[:4], refs[4:8]
    (
        img_kept, txt_kept, scalars, image_head, text_head,
        loss, grad_images, grad_texts, grad_scale, grad_bias,
        img_frames, txt_frames, cosines, matches, image_out, text_out,
        loss_out, scale_out, bias_out, sems,
    ) = refs[8:]
    rows, width = img_kept.shape[0], img_kept.shape[1] - LANES
    frame_rows, groups = 2 * rows, 2 * rows // TILE
    blocks = width // LANES + 1
    device = lax.axis_index("dev")
    odd, chip = lax.rem(device, 2), device // 2
    depth = chips.bit_length() - 1
    scale, bias = scalars[0, :1, :1], scalars[1, :1, :1]

    position = lax.broadcasted_iota(jnp.int32, (frame_rows, LANES), 0)
    lane = lax.broadcasted_iota(jnp.int32, (frame_rows, LANES), 1)
    from_mine = (position < rows) == (odd == 0)

    def assemble(held, passed):
        for apart in range(chips):
            target = jnp.bitwise_xor(chip, apart)
            flip = apart.bit_count() % 2 == 1
            (mine, slot), (other, other_slot) = (
                (pieces[slot % 4], slot // 4)
                for pieces, slot in (
                    (mine_pieces, slot_of(2 * apart, held)),
                    (other_pieces, slot_of(2 * apart, passed)),
                )
            )
            for block in range(blocks):
                columns = slice(block * LANES, (block + 1) * LANES)
                a = frame_of(mine, slot, block, groups, lane)
                b = frame_of(other, other_slot, block, groups, lane)
                a, b = (b, a) if flip else (a, b)
                img_frames[target, :, columns] = jnp.where(from_mine, a, b).astype(jnp.bfloat16)
                txt_frames[target, :, columns] = jnp.where(from_mine, b, a).astype(jnp.bfloat16)

    kind = parity(device, depth + 1)
    pl.when(kind == 0)(functools.partial(assemble, orders[0], orders[1]))
    pl.when(kind == 1)(functools.partial(assemble, orders[1], orders[0]))
    flat = (chips * frame_rows, blocks * LANES)
    img_all, txt_all = img_frames[...].reshape(flat), txt_frames[...].reshape(flat)

    img_emb, txt_emb = img_all[:, :width], txt_all[:, :width]
    img_ids, txt_ids = img_all[:, width:], txt_all[:, width:]
    cosines[...] = contract_last(img_emb, txt_emb)
    matches[...] = contract_last(img_ids, txt_ids)

    def own_rows(rows_of_chip, late):
        return jnp.where(late, rows_of_chip[rows:], rows_of_chip[:rows])

    here = pl.ds(pl.multiple_of(chip * frame_rows, TILE), frame_rows)
    own_txt_ids = own_rows(txt_frames[chip, :, width:].astype(jnp.float32), odd == 0)
    txt_unit = txt_kept[:, :width].astype(jnp.bfloat16)
    projected = []
    for kept, cosine, match, others in (
        (img_kept, own_rows(cosines[here], odd == 1), own_rows(matches[here], odd == 1), txt_emb),
        (
            txt_kept,
            contract_last(txt_unit, img_emb),
            contract_last(own_txt_ids.astype(jnp.bfloat16), img_ids),
            img_emb,
        ),
    ):
        unit, length = kept[:, :width], kept[:, width : width + 1]
        slopes = pair_terms(cosine, match, scale, bias)[2].astype(jnp.bfloat16)
        grad = scale * jnp.dot(slopes, others, preferred_element_type=jnp.float32)
        inner = jnp.sum(unit * grad, axis=1, keepdims=True)
        projected.append(((grad - unit * inner) / length).astype(jnp.bfloat16))

    def back(side, head, out, at=slice(None)):
        out[:, at] = contract_last(projected[side], head[at]).astype(jnp.bfloat16)

    def gather_sums(low, high, sums):
        for strip in range(low, high, TILE):
            strip_rows = slice(strip, strip + TILE)
            cosine = cosines[strip_rows]
            negative, decay, slopes = pair_terms(cosine, matches[strip_rows], scale, bias)
            terms = (jnp.maximum(negative, 0.0) + jnp.log1p(decay), slopes * cosine, slopes)
            sums = tuple(total + term for total, term in zip(sums, terms))
        return sums

    sums = (jnp.zeros((TILE, pairs), jnp.float32),) * 3
    copies = [
        pltpu.make_async_copy(image_out, grad_images, sems.at[0]),
        pltpu.make_async_copy(text_out, grad_texts, sems.at[1]),
        pltpu.make_async_copy(loss_out, loss, sems.at[2]),
        pltpu.make_async_copy(scale_out, grad_scale, sems.at[3]),
        pltpu.make_async_copy(bias_out, grad_bias, sems.at[4]),
    ]
    back(0, image_head, image_out)
    copies[0].start()
    back(1, text_head, text_out)
    copies[1].start()
    sums = gather_sums(0, pairs, sums)
    totals = [jnp.sum(total, keepdims=True) / pairs for total in sums]
    loss_out[0] = totals[0][0, 0]
    scale_out[0] = (scale * totals[1])[0, 0]
    bias_out[0] = totals[2][0, 0]
    for copy in copies[2:]:
        copy.start()
    for copy in copies:
        copy.wait()


def fetch_kernel(image_head, text_head, new, image_held, text_held, sems):
    copies = [
        pltpu.make_async_copy(image_head, image_held, sems.at[0]),
        pltpu.make_async_copy(text_head, text_held, sems.at[1]),
    ]
    for copy in copies:
        copy.start()
    for copy in copies:
        copy.wait()


def scalar_kernel(log_scale, logit_bias, payload, scalars):
    scalars[0] = jnp.exp(jnp.full(scalars.shape[1:], log_scale[0], jnp.float32))
    scalars[1] = jnp.full(scalars.shape[1:], logit_bias[0], jnp.float32)


def on_device_small(
    image_feats, text_feats, image_head, text_head, log_scale, logit_bias, image_group, text_group
):
    devices = lax.axis_size("dev")
    chips = devices // 2
    rows, depth = image_feats.shape
    width = image_head.shape[1]
    blocks = width // LANES + 1
    tiles = 2 * rows // TILE * (width // LANES) + 1
    chunks = next(c for c in (1,) if depth % (c * LANES) == 0 or c == 1)
    vmem, smem, hbm = (
        pl.BlockSpec(memory_space=pltpu.VMEM),
        pl.BlockSpec(memory_space=pltpu.SMEM),
        pl.BlockSpec(memory_space=pltpu.HBM),
    )
    f32, bf16 = jnp.float32, jnp.bfloat16
    payload, img_kept, txt_kept = pl.pallas_call(
        project_kernel,
        out_shape=(
            jax.ShapeDtypeStruct((tiles, TILE, LANES), bf16),
            jax.ShapeDtypeStruct((rows, width + LANES), f32),
            jax.ShapeDtypeStruct((rows, width + LANES), f32),
        ),
        in_specs=[hbm] * 6,
        out_specs=(vmem,) * 3,
        scratch_shapes=[
            pltpu.VMEM((depth, width), bf16),
            pltpu.VMEM((depth, width), bf16),
            pltpu.VMEM((2 * rows, width), f32),
            pltpu.VMEM((rows, depth), bf16),
            pltpu.VMEM((rows, depth), bf16),
            pltpu.SMEM((rows,), jnp.int32),
            pltpu.SMEM((rows,), jnp.int32),
            pltpu.SemaphoreType.DMA((2, chunks)),
            pltpu.SemaphoreType.DMA((4,)),
        ],
        compiler_params=pltpu.CompilerParams(vmem_limit_bytes=16 << 20),
        name="project",
    )(
        *(
            pltpu.with_memory_space_constraint(array, pltpu.HBM)
            for array in (image_group, text_group, image_feats, text_feats, image_head, text_head)
        )
    )

    orders = hop_orders(devices)
    bits = devices.bit_length() - 1

    def swap(array):
        return lax.ppermute(array, "dev", [(i, i ^ 1) for i in range(devices)])

    def hop(array, level):
        pairs = [(i, i ^ orders[parity(i, bits)][level] ^ 1) for i in range(devices)]
        return lax.ppermute(array, "dev", pairs)

    scalars = pl.pallas_call(
        scalar_kernel,
        out_shape=jax.ShapeDtypeStruct((2, TILE, LANES), f32),
        in_specs=[smem, smem, pl.BlockSpec(memory_space=pl.ANY)],
        out_specs=vmem,
        cost_estimate=pl.CostEstimate(flops=SIDE_FLOPS, bytes_accessed=64, transcendentals=0),
        compiler_params=pltpu.CompilerParams(vmem_limit_bytes=1 << 20),
        name="scalars",
    )(log_scale.reshape(1), logit_bias.reshape(1), payload)
    old = payload[None]
    for level in range(bits - 3):
        old = jnp.concatenate([old, hop(old, level)], axis=0)
        if level == 0:
            old, scalars = lax.optimization_barrier((old, scalars))
    new = hop(old, bits - 3)
    old_far = hop(old, bits - 2)
    new_far = hop(new, bits - 2)
    image_held, text_held = pl.pallas_call(
        fetch_kernel,
        out_shape=(jax.ShapeDtypeStruct((depth, width), bf16),) * 2,
        in_specs=[hbm, hbm, pl.BlockSpec(memory_space=pl.ANY)],
        out_specs=(vmem,) * 2,
        scratch_shapes=[pltpu.SemaphoreType.DMA((2,))],
        cost_estimate=pl.CostEstimate(
            flops=SIDE_FLOPS, bytes_accessed=4 * depth * width, transcendentals=0
        ),
        compiler_params=pltpu.CompilerParams(vmem_limit_bytes=8 << 20),
        name="fetch",
    )(
        pltpu.with_memory_space_constraint(image_head, pltpu.HBM),
        pltpu.with_memory_space_constraint(text_head, pltpu.HBM),
        new,
    )
    old_other = swap(old)
    new_other = swap(new)
    old_far_other = swap(old_far)
    new_far, image_held, text_held, old_other, new_other, old_far_other = lax.optimization_barrier(
        (new_far, image_held, text_held, old_other, new_other, old_far_other)
    )
    new_far_other = swap(new_far)
    pieces = (old, old_far, new, new_far, old_other, old_far_other, new_other, new_far_other)

    loss, grad_images, grad_texts, grad_scale, grad_bias = pl.pallas_call(
        functools.partial(loss_kernel, chips, rows * devices, orders),
        out_shape=(
            jax.ShapeDtypeStruct((1,), f32),
            jax.ShapeDtypeStruct((rows, depth), bf16),
            jax.ShapeDtypeStruct((rows, depth), bf16),
            jax.ShapeDtypeStruct((1,), f32),
            jax.ShapeDtypeStruct((1,), f32),
        ),
        in_specs=[vmem] * 13,
        out_specs=(hbm,) * 5,
        scratch_shapes=[pltpu.VMEM((chips, 2 * rows, blocks * LANES), bf16)] * 2
        + [pltpu.VMEM((rows * devices, rows * devices), f32)] * 2
        + [pltpu.VMEM((rows, depth), bf16)] * 2
        + [pltpu.SMEM((1,), f32)] * 3
        + [pltpu.SemaphoreType.DMA((5,))],
        compiler_params=pltpu.CompilerParams(vmem_limit_bytes=24 << 20),
        name="loss",
    )(
        *(
            pltpu.with_memory_space_constraint(array, pltpu.VMEM)
            for array in pieces
            + (img_kept, txt_kept, scalars, image_held, text_held)
        )
    )
    return (loss[0], grad_images, grad_texts, grad_scale[0], grad_bias[0])


def on_device(image_feats, text_feats, image_head, *rest):
    devices = lax.axis_size("dev")
    pairs = image_feats.shape[0] * devices
    small = (
        4 * pairs * pairs <= LOGIT_BUDGET
        and devices >= 8
        and devices & (devices - 1) == 0
        and image_head.shape[1] % LANES == 0
        and 2 * image_feats.shape[0] % TILE == 0
        and 2 * image_feats.shape[0] // TILE * BITS <= LANES
    )
    body = on_device_small if small else on_device_large
    return body(image_feats, text_feats, image_head, *rest)


def solution(mesh):
    placed = (P("dev", None), P("dev", None), P(), P(), P(), P(), P("dev"), P("dev"))
    return jax.shard_map(
        on_device,
        mesh=mesh,
        in_specs=placed,
        out_specs=(P(), P("dev", None), P("dev", None), P(), P()),
        check_vma=False,
    )
```

profile of v0, /device:TPU:31, one launch (start us, length us, event | category | flops | bytes accessed | tf_op | source)
XLA Modules:
  0.0 27.2 jit_solution(17418540565198552941)
XLA Ops:
  0.6 2.4 %project.1 = (bf16[16,8,128]{2,1,0:T(8,128)(2,1)S(1)}, f32[12,768]{1,0:T(8,128)S(1)}, f32[12,768]{1,0:T(8,128)S(1)}) custom-call(s32[12]{0:T(128)} %image_ids.1, s32[12]{0:T(128)} %text_ids.1, bf16[12,1152]{1,0:T(8,128)(2,1)} %image_feats.1, bf16[12,1152]{1,0:T(8,128)(2,1)} %text_feats.1, bf16[1152,640]{1,0:T(8,128)(2,1)} %image_head.3, ...), custom_call_target="tpu_custom_call" | custom-call | tf_op jit(solution)/shard_map/project/pallas_call | solution.py:326
  3.0 0.7 %collective-permute-start = (bf16[1,16,8,128]{3,2,1,0:T(8,128)(2,1)S(1)}, bf16[1,16,8,128]{3,2,1,0:T(8,128)(2,1)S(1)}, u32[]{:S(2)}, u32[]{:S(2)}) collective-permute-start(bf16[1,16,8,128]{3,2,1,0:T(8,128)(2,1)S(1)} %bitcast.8), channel_id=1, source_target_pairs={{0,17},{1,16},{2,19},{3,18},{4,21},{5,20},{6,23},{7,22},{8,25},{9,... | collective-permute-start | bytes 98312 | tf_op jit(solution)/shard_map/ppermute | solution.py:363
  5.0 3.5 %collective-permute-done = bf16[1,16,8,128]{3,2,1,0:T(8,128)(2,1)S(1)} collective-permute-done((bf16[1,16,8,128]{3,2,1,0:T(8,128)(2,1)S(1)}, bf16[1,16,8,128]{3,2,1,0:T(8,128)(2,1)S(1)}, u32[]{:S(2)}, u32[]{:S(2)}) %collective-permute-start) | collective-permute-done | bytes 32800 | tf_op jit(solution)/shard_map/ppermute | solution.py:363
  8.5 0.6 %collective-permute-start.1 = (bf16[2,16,8,128]{3,2,1,0:T(8,128)(2,1)S(1)}, bf16[2,16,8,128]{3,2,1,0:T(8,128)(2,1)S(1)}, u32[]{:S(2)}, u32[]{:S(2)}) collective-permute-start(bf16[2,16,8,128]{3,2,1,0:T(8,128)(2,1)S(1)} %pad_maximum_fusion), channel_id=1, source_target_pairs={{0,9},{1,4},{2,7},{3,10},{4,1},{5,12},{6,15},{7,2},{8,13},{9,0},{1... | collective-permute-start | bytes 196616 | tf_op jit(solution)/shard_map/ppermute | solution.py:363
  9.1 3.2 %collective-permute-done.1 = bf16[2,16,8,128]{3,2,1,0:T(8,128)(2,1)S(1)} collective-permute-done((bf16[2,16,8,128]{3,2,1,0:T(8,128)(2,1)S(1)}, bf16[2,16,8,128]{3,2,1,0:T(8,128)(2,1)S(1)}, u32[]{:S(2)}, u32[]{:S(2)}) %collective-permute-start.1) | collective-permute-done | bytes 65568 | tf_op jit(solution)/shard_map/ppermute | solution.py:363
  12.3 0.6 %collective-permute-start.3 = (bf16[4,16,8,128]{3,2,1,0:T(8,128)(2,1)S(1)}, bf16[4,16,8,128]{3,2,1,0:T(8,128)(2,1)S(1)}, u32[]{:S(2)}, u32[]{:S(2)}) collective-permute-start(bf16[4,16,8,128]{3,2,1,0:T(8,128)(2,1)S(1)} %constant_dynamic-update-slice_fusion.refs_0_), channel_id=1, source_target_pairs={{0,5},{1,2},{2,1},{3,6},{4,7},{5,0},{6,3},{7,4},{8,11},{9,12},{10,... | collective-permute-start | bytes 393224 | tf_op jit(solution)/shard_map/ppermute | solution.py:363
  12.9 0.0 collective-permute-start.2
  12.9 0.6 %collective-permute-start.5 = (bf16[4,16,8,128]{3,2,1,0:T(8,128)(2,1)S(1)}, bf16[4,16,8,128]{3,2,1,0:T(8,128)(2,1)S(1)}, u32[]{:S(2)}, u32[]{:S(2)}) collective-permute-start(bf16[4,16,8,128]{3,2,1,0:T(8,128)(2,1)S(1)} %constant_dynamic-update-slice_fusion.refs_0_), channel_id=1, source_target_pairs={{0,1},{1,0},{2,3},{3,2},{4,5},{5,4},{6,7},{7,6},{8,9},{9,8},{10,11... | collective-permute-start | bytes 393224 | tf_op jit(solution)/shard_map/ppermute | solution.py:359
  13.5 4.8 %collective-permute-done.3.new.refs_2_ = bf16[4,16,8,128]{3,2,1,0:T(8,128)(2,1)S(1)} collective-permute-done((bf16[4,16,8,128]{3,2,1,0:T(8,128)(2,1)S(1)}, bf16[4,16,8,128]{3,2,1,0:T(8,128)(2,1)S(1)}, u32[]{:S(2)}, u32[]{:S(2)}) %collective-permute-start.3) | collective-permute-done | bytes 131104 | tf_op jit(solution)/shard_map/ppermute | solution.py:363
  18.3 0.0 collective-permute-start.6
  18.3 0.0 collective-permute-start.4
  18.4 0.0 collective-permute-done.2.refs_1_
  18.4 0.5 %collective-permute-start.7 = (bf16[4,16,8,128]{3,2,1,0:T(8,128)(2,1)S(1)}, bf16[4,16,8,128]{3,2,1,0:T(8,128)(2,1)S(1)}, u32[]{:S(2)}, u32[]{:S(2)}) collective-permute-start(bf16[4,16,8,128]{3,2,1,0:T(8,128)(2,1)S(1)} %collective-permute-done.2.refs_1_), channel_id=1, source_target_pairs={{0,1},{1,0},{2,3},{3,2},{4,5},{5,4},{6,7},{7,6},{8,9},{9,8},{10,11... | collective-permute-start | bytes 393224 | tf_op jit(solution)/shard_map/ppermute | solution.py:359
  18.9 1.8 %fetch.1 = (bf16[1152,640]{1,0:T(8,128)(2,1)S(1)}, bf16[1152,640]{1,0:T(8,128)(2,1)S(1)}) custom-call(bf16[1152,640]{1,0:T(8,128)(2,1)} %image_head.3, bf16[1152,640]{1,0:T(8,128)(2,1)} %text_head.3, bf16[4,16,8,128]{3,2,1,0:T(8,128)(2,1)S(1)} %collective-permute-done.3.new.refs_2_), custom_call_target="tpu_custom_call" | custom-call | flops 67108864 | bytes 2949120 | tf_op jit(solution)/shard_map/fetch/pallas_call | solution.py:382
  20.7 0.0 collective-permute-done.5.refs_4_
  20.7 0.0 collective-permute-done.6.refs_6_
  20.7 2.1 %collective-permute-done.4.refs_3_ = bf16[4,16,8,128]{3,2,1,0:T(8,128)(2,1)S(1)} collective-permute-done((bf16[4,16,8,128]{3,2,1,0:T(8,128)(2,1)S(1)}, bf16[4,16,8,128]{3,2,1,0:T(8,128)(2,1)S(1)}, u32[]{:S(2)}, u32[]{:S(2)}) %collective-permute-start.4) | collective-permute-done | bytes 131104 | tf_op jit(solution)/shard_map/ppermute | solution.py:363
  22.9 0.0 collective-permute-done.7.refs_5_
  22.9 0.4 %collective-permute-start.8 = (bf16[4,16,8,128]{3,2,1,0:T(8,128)(2,1)S(1)}, bf16[4,16,8,128]{3,2,1,0:T(8,128)(2,1)S(1)}, u32[]{:S(2)}, u32[]{:S(2)}) collective-permute-start(bf16[4,16,8,128]{3,2,1,0:T(8,128)(2,1)S(1)} %collective-permute-done.4.refs_3_), channel_id=1, source_target_pairs={{0,1},{1,0},{2,3},{3,2},{4,5},{5,4},{6,7},{7,6},{8,9},{9,8},{10,11... | collective-permute-start | bytes 393224 | tf_op jit(solution)/shard_map/ppermute | solution.py:359
  23.3 1.0 %collective-permute-done.8.refs_7_ = bf16[4,16,8,128]{3,2,1,0:T(8,128)(2,1)S(1)} collective-permute-done((bf16[4,16,8,128]{3,2,1,0:T(8,128)(2,1)S(1)}, bf16[4,16,8,128]{3,2,1,0:T(8,128)(2,1)S(1)}, u32[]{:S(2)}, u32[]{:S(2)}) %collective-permute-start.8) | collective-permute-done | bytes 131104 | tf_op jit(solution)/shard_map/ppermute | solution.py:359
  24.2 2.9 %loss.1 = (f32[1]{0:T(128)}, bf16[12,1152]{1,0:T(8,128)(2,1)}, bf16[12,1152]{1,0:T(8,128)(2,1)}, f32[1]{0:T(128)}, f32[1]{0:T(128)}) custom-call(bf16[4,16,8,128]{3,2,1,0:T(8,128)(2,1)S(1)} %constant_dynamic-update-slice_fusion.refs_0_, bf16[4,16,8,128]{3,2,1,0:T(8,128)(2,1)S(1)} %collective-permute-done.2.refs_1_, ...), custom_call_target="tpu_custom_call" | custom-call | tf_op jit(solution)/shard_map/loss/pallas_call | solution.py:407
  (4 shorter events, 0.0 us)
Async XLA Ops:
  3.0 5.5 %collective-permute-start = (bf16[1,16,8,128]{3,2,1,0:T(8,128)(2,1)S(1)}, bf16[1,16,8,128]{3,2,1,0:T(8,128)(2,1)S(1)}, u32[]{:S(2)}, u32[]{:S(2)}) collective-permute-start(bf16[1,16,8,128]{3,2,1,0:T(8,128)(2,1)S(1)} %bitcast.8), channel_id=1, source_target_pairs={{0,17},{1,16},{2,19},{3,18},{4,21},{5,20},{6,23},{7,22},{8,25},{9,... | collective-permute-start | bytes 98312 | tf_op jit(solution)/shard_map/ppermute | solution.py:363
  8.5 3.8 %collective-permute-start.1 = (bf16[2,16,8,128]{3,2,1,0:T(8,128)(2,1)S(1)}, bf16[2,16,8,128]{3,2,1,0:T(8,128)(2,1)S(1)}, u32[]{:S(2)}, u32[]{:S(2)}) collective-permute-start(bf16[2,16,8,128]{3,2,1,0:T(8,128)(2,1)S(1)} %pad_maximum_fusion), channel_id=1, source_target_pairs={{0,9},{1,4},{2,7},{3,10},{4,1},{5,12},{6,15},{7,2},{8,13},{9,0},{1... | collective-permute-start | bytes 196616 | tf_op jit(solution)/shard_map/ppermute | solution.py:363
  12.3 6.0 %collective-permute-start.3 = (bf16[4,16,8,128]{3,2,1,0:T(8,128)(2,1)S(1)}, bf16[4,16,8,128]{3,2,1,0:T(8,128)(2,1)S(1)}, u32[]{:S(2)}, u32[]{:S(2)}) collective-permute-start(bf16[4,16,8,128]{3,2,1,0:T(8,128)(2,1)S(1)} %constant_dynamic-update-slice_fusion.refs_0_), channel_id=1, source_target_pairs={{0,5},{1,2},{2,1},{3,6},{4,7},{5,0},{6,3},{7,4},{8,11},{9,12},{10,... | collective-permute-start | bytes 393224 | tf_op jit(solution)/shard_map/ppermute | solution.py:363
  12.9 5.4 %collective-permute-start.2 = (bf16[4,16,8,128]{3,2,1,0:T(8,128)(2,1)S(1)}, bf16[4,16,8,128]{3,2,1,0:T(8,128)(2,1)S(1)}, u32[]{:S(2)}, u32[]{:S(2)}) collective-permute-start(bf16[4,16,8,128]{3,2,1,0:T(8,128)(2,1)S(1)} %constant_dynamic-update-slice_fusion.refs_0_), channel_id=1, source_target_pairs={{0,3},{1,8},{2,11},{3,0},{4,13},{5,6},{6,5},{7,14},{8,1},{9,10},{1... | collective-permute-start | bytes 393224 | tf_op jit(solution)/shard_map/ppermute | solution.py:363
  12.9 7.8 %collective-permute-start.5 = (bf16[4,16,8,128]{3,2,1,0:T(8,128)(2,1)S(1)}, bf16[4,16,8,128]{3,2,1,0:T(8,128)(2,1)S(1)}, u32[]{:S(2)}, u32[]{:S(2)}) collective-permute-start(bf16[4,16,8,128]{3,2,1,0:T(8,128)(2,1)S(1)} %constant_dynamic-update-slice_fusion.refs_0_), channel_id=1, source_target_pairs={{0,1},{1,0},{2,3},{3,2},{4,5},{5,4},{6,7},{7,6},{8,9},{9,8},{10,11... | collective-permute-start | bytes 393224 | tf_op jit(solution)/shard_map/ppermute | solution.py:359
  18.3 2.4 %collective-permute-start.6 = (bf16[4,16,8,128]{3,2,1,0:T(8,128)(2,1)S(1)}, bf16[4,16,8,128]{3,2,1,0:T(8,128)(2,1)S(1)}, u32[]{:S(2)}, u32[]{:S(2)}) collective-permute-start(bf16[4,16,8,128]{3,2,1,0:T(8,128)(2,1)S(1)} %collective-permute-done.3.new.refs_2_), channel_id=1, source_target_pairs={{0,1},{1,0},{2,3},{3,2},{4,5},{5,4},{6,7},{7,6},{8,9},{9,8},{10,11... | collective-permute-start | bytes 393224 | tf_op jit(solution)/shard_map/ppermute | solution.py:359
  18.3 4.5 %collective-permute-start.4 = (bf16[4,16,8,128]{3,2,1,0:T(8,128)(2,1)S(1)}, bf16[4,16,8,128]{3,2,1,0:T(8,128)(2,1)S(1)}, u32[]{:S(2)}, u32[]{:S(2)}) collective-permute-start(bf16[4,16,8,128]{3,2,1,0:T(8,128)(2,1)S(1)} %collective-permute-done.3.new.refs_2_), channel_id=1, source_target_pairs={{0,3},{1,8},{2,11},{3,0},{4,13},{5,6},{6,5},{7,14},{8,1},{9,10},{1... | collective-permute-start | bytes 393224 | tf_op jit(solution)/shard_map/ppermute | solution.py:363
  18.4 4.5 %collective-permute-start.7 = (bf16[4,16,8,128]{3,2,1,0:T(8,128)(2,1)S(1)}, bf16[4,16,8,128]{3,2,1,0:T(8,128)(2,1)S(1)}, u32[]{:S(2)}, u32[]{:S(2)}) collective-permute-start(bf16[4,16,8,128]{3,2,1,0:T(8,128)(2,1)S(1)} %collective-permute-done.2.refs_1_), channel_id=1, source_target_pairs={{0,1},{1,0},{2,3},{3,2},{4,5},{5,4},{6,7},{7,6},{8,9},{9,8},{10,11... | collective-permute-start | bytes 393224 | tf_op jit(solution)/shard_map/ppermute | solution.py:359
  22.9 1.4 %collective-permute-start.8 = (bf16[4,16,8,128]{3,2,1,0:T(8,128)(2,1)S(1)}, bf16[4,16,8,128]{3,2,1,0:T(8,128)(2,1)S(1)}, u32[]{:S(2)}, u32[]{:S(2)}) collective-permute-start(bf16[4,16,8,128]{3,2,1,0:T(8,128)(2,1)S(1)} %collective-permute-done.4.refs_3_), channel_id=1, source_target_pairs={{0,1},{1,0},{2,3},{3,2},{4,5},{5,4},{6,7},{7,6},{8,9},{9,8},{10,11... | collective-permute-start | bytes 393224 | tf_op jit(solution)/shard_map/ppermute | solution.py:359
where the time goes:
time: 27.4 us; the launch traced here: 27.2 us
  waiting for transfers between devices  14.6 us (53%)
  Pallas kernels  7.14 us (26%)
  starting transfers between devices  3.39 us (12%)
  between operations  1.98 us (7%)
    ppermute x5, waiting for transfers between devices, hop(): return lax.ppermute(array, 'dev', pairs)  13.6 us
    pallas_call x1, Pallas kernels, on_device_small(): pl.pallas_call(functools.partial(loss_kernel, chips, rows * devices, orde...  2.92 us
    pallas_call x1, Pallas kernels, on_device_small(): pl.pallas_call(project_kernel, out_shape=(jax.ShapeDtypeStruct((tiles, TI...  2.38 us
    ppermute x5, starting transfers between devices, hop(): return lax.ppermute(array, 'dev', pairs)  1.86 us
    pallas_call x1, Pallas kernels, on_device_small(): pl.pallas_call(fetch_kernel, out_shape=(jax.ShapeDtypeStruct((depth, widt...  1.83 us
    ppermute x4, starting transfers between devices, swap(): return lax.ppermute(array, 'dev', [(i, i ^ 1) for i in range(devices)])  1.52 us
    ppermute x4, waiting for transfers between devices, swap(): return lax.ppermute(array, 'dev', [(i, i ^ 1) for i in range(devices)])  0.99 us
  transfers between devices with their start and end apart: 9, of which 5 were waited for; matrix products, arithmetic and copies ran while one was open for 0% of the time, Pallas kernels for 7%

commit v1 on v0

--- a/solution.py
+++ b/solution.py
@@ -152,7 +152,7 @@
 def hop_orders(devices):
     bits = [1 << level for level in reversed(range(1, devices.bit_length() - 1))]
     first, rest = bits[:1], bits[1:]
-    return first + rest, first + rest[1:] + rest[:1]
+    return first + rest, first + [rest[2], rest[0], rest[1]]
 
 
 def parity(number, bits):
@@ -371,14 +371,21 @@
         compiler_params=pltpu.CompilerParams(vmem_limit_bytes=1 << 20),
         name="scalars",
     )(log_scale.reshape(1), logit_bias.reshape(1), payload)
-    old = payload[None]
-    for level in range(bits - 3):
-        old = jnp.concatenate([old, hop(old, level)], axis=0)
-        if level == 0:
-            old, scalars = lax.optimization_barrier((old, scalars))
-    new = hop(old, bits - 3)
-    old_far = hop(old, bits - 2)
-    new_far = hop(new, bits - 2)
+
+    def grow(first, level):
+        early = hop(first[0], level)
+        late = hop(first[1], level)
+        return jnp.concatenate([early, late], axis=0)
+
+    own = payload[None]
+    one = hop(own, 0)
+    one, scalars = lax.optimization_barrier((one, scalars))
+    pair = jnp.concatenate([own, one], axis=0)
+    two = hop(pair, 1)
+    old = jnp.concatenate([pair, two], axis=0)
+    new = grow((pair, two), 2)
+    old_far = hop(old, 3)
+    new_far = hop(new, 3)
     image_held, text_held = pl.pallas_call(
         fetch_kernel,
         out_shape=(jax.ShapeDtypeStruct((depth, width), bf16),) * 2,

time: 27.4 us -> 27.6 us (level)
  the two profiles are of different devices: /device:TPU:31 before, /device:TPU:25 now
where the time goes in v1:
time: 27.6 us; the launch traced here: 27.4 us
  waiting for transfers between devices  12.4 us (45%)
  Pallas kernels  7.14 us (26%)
  starting transfers between devices  5.83 us (21%)
  between operations  1.99 us (7%)
    ppermute x6, waiting for transfers between devices, hop(): return lax.ppermute(array, 'dev', pairs)  11.2 us
    ppermute x6, starting transfers between devices, hop(): return lax.ppermute(array, 'dev', pairs)  4.22 us
    pallas_call x1, Pallas kernels, on_device_small(): pl.pallas_call(functools.partial(loss_kernel, chips, rows * devices, orde...  2.92 us
    pallas_call x1, Pallas kernels, on_device_small(): pl.pallas_call(project_kernel, out_shape=(jax.ShapeDtypeStruct((tiles, TI...  2.38 us
    pallas_call x1, Pallas kernels, on_device_small(): pl.pallas_call(fetch_kernel, out_shape=(jax.ShapeDtypeStruct((depth, widt...  1.83 us
    ppermute x4, starting transfers between devices, swap(): return lax.ppermute(array, 'dev', [(i, i ^ 1) for i in range(devices)])  1.61 us
    ppermute x4, waiting for transfers between devices, swap(): return lax.ppermute(array, 'dev', [(i, i ^ 1) for i in range(devices)])  1.28 us
  transfers between devices with their start and end apart: 10, of which 5 were waited for; matrix products, arithmetic and copies ran while one was open for 0% of the time, Pallas kernels for 7%

profile of v1, /device:TPU:25, one launch (start us, length us, event | category | flops | bytes accessed | tf_op | source)
XLA Modules:
  0.0 27.4 jit_solution(13065553776063879875)
XLA Ops:
  0.6 2.4 %project.1 = (bf16[16,8,128]{2,1,0:T(8,128)(2,1)S(1)}, f32[12,768]{1,0:T(8,128)S(1)}, f32[12,768]{1,0:T(8,128)S(1)}) custom-call(s32[12]{0:T(128)} %image_ids.1, s32[12]{0:T(128)} %text_ids.1, bf16[12,1152]{1,0:T(8,128)(2,1)} %image_feats.1, bf16[12,1152]{1,0:T(8,128)(2,1)} %text_feats.1, bf16[1152,640]{1,0:T(8,128)(2,1)} %image_head.3, ...), custom_call_target="tpu_custom_call" | custom-call | tf_op jit(solution)/shard_map/project/pallas_call | solution.py:326
  3.0 0.7 %collective-permute-start = (bf16[1,16,8,128]{3,2,1,0:T(8,128)(2,1)S(1)}, bf16[1,16,8,128]{3,2,1,0:T(8,128)(2,1)S(1)}, u32[]{:S(2)}, u32[]{:S(2)}) collective-permute-start(bf16[1,16,8,128]{3,2,1,0:T(8,128)(2,1)S(1)} %bitcast.8), channel_id=1, source_target_pairs={{0,17},{1,16},{2,19},{3,18},{4,21},{5,20},{6,23},{7,22},{8,25},{9,... | collective-permute-start | bytes 98312 | tf_op jit(solution)/shard_map/ppermute | solution.py:363
  5.0 3.5 %collective-permute-done = bf16[1,16,8,128]{3,2,1,0:T(8,128)(2,1)S(1)} collective-permute-done((bf16[1,16,8,128]{3,2,1,0:T(8,128)(2,1)S(1)}, bf16[1,16,8,128]{3,2,1,0:T(8,128)(2,1)S(1)}, u32[]{:S(2)}, u32[]{:S(2)}) %collective-permute-start) | collective-permute-done | bytes 32800 | tf_op jit(solution)/shard_map/ppermute | solution.py:363
  8.5 1.6 %collective-permute-start.1 = (bf16[2,16,8,128]{3,2,1,0:T(8,128)(2,1)S(1)}, bf16[2,16,8,128]{3,2,1,0:T(8,128)(2,1)S(1)}, u32[]{:S(2)}, u32[]{:S(2)}) collective-permute-start(bf16[2,16,8,128]{3,2,1,0:T(8,128)(2,1)S(1)} %pad_maximum_fusion.1), channel_id=1, source_target_pairs={{0,9},{1,2},{2,1},{3,10},{4,7},{5,12},{6,15},{7,4},{8,11},{9,0},{1... | collective-permute-start | bytes 196616 | tf_op jit(solution)/shard_map/ppermute | solution.py:363
  10.1 0.0 collective-permute-start.3
  10.1 2.3 %collective-permute-done.1 = bf16[2,16,8,128]{3,2,1,0:T(8,128)(2,1)S(1)} collective-permute-done((bf16[2,16,8,128]{3,2,1,0:T(8,128)(2,1)S(1)}, bf16[2,16,8,128]{3,2,1,0:T(8,128)(2,1)S(1)}, u32[]{:S(2)}, u32[]{:S(2)}) %collective-permute-start.1) | collective-permute-done | bytes 65568 | tf_op jit(solution)/shard_map/ppermute | solution.py:363
  12.4 0.4 %collective-permute-start.6 = (bf16[4,16,8,128]{3,2,1,0:T(8,128)(2,1)S(1)}, bf16[4,16,8,128]{3,2,1,0:T(8,128)(2,1)S(1)}, u32[]{:S(2)}, u32[]{:S(2)}) collective-permute-start(bf16[4,16,8,128]{3,2,1,0:T(8,128)(2,1)S(1)} %pad_maximum_fusion.refs_0_), channel_id=1, source_target_pairs={{0,1},{1,0},{2,3},{3,2},{4,5},{5,4},{6,7},{7,6},{8,9},{9,8},{10,11... | collective-permute-start | bytes 393224 | tf_op jit(solution)/shard_map/ppermute | solution.py:359
  12.8 1.2 %collective-permute-start.2 = (bf16[4,16,8,128]{3,2,1,0:T(8,128)(2,1)S(1)}, bf16[4,16,8,128]{3,2,1,0:T(8,128)(2,1)S(1)}, u32[]{:S(2)}, u32[]{:S(2)}) collective-permute-start(bf16[4,16,8,128]{3,2,1,0:T(8,128)(2,1)S(1)} %pad_maximum_fusion.refs_0_), channel_id=1, source_target_pairs={{0,3},{1,4},{2,7},{3,0},{4,1},{5,6},{6,5},{7,2},{8,13},{9,10},{10,... | collective-permute-start | bytes 393224 | tf_op jit(solution)/shard_map/ppermute | solution.py:363
  14.0 0.0 collective-permute-start.4
  14.0 0.0 collective-permute-done.3
  14.0 4.0 %collective-permute-done.4 = bf16[2,16,8,128]{3,2,1,0:T(8,128)(2,1)S(1)} collective-permute-done((bf16[2,16,8,128]{3,2,1,0:T(8,128)(2,1)S(1)}, bf16[2,16,8,128]{3,2,1,0:T(8,128)(2,1)S(1)}, u32[]{:S(2)}, u32[]{:S(2)}) %collective-permute-start.4) | collective-permute-done | bytes 65568 | tf_op jit(solution)/shard_map/ppermute | solution.py:363
  18.0 0.7 %collective-permute-start.7 = (bf16[4,16,8,128]{3,2,1,0:T(8,128)(2,1)S(1)}, bf16[4,16,8,128]{3,2,1,0:T(8,128)(2,1)S(1)}, u32[]{:S(2)}, u32[]{:S(2)}) collective-permute-start(bf16[4,16,8,128]{3,2,1,0:T(8,128)(2,1)S(1)} %constant_dynamic-update-slice_fusion.new.refs_2_), channel_id=1, source_target_pairs={{0,1},{1,0},{2,3},{3,2},{4,5},{5,4},{6,7},{7,6},{8,9},{9,8},{10,11... | collective-permute-start | bytes 393224 | tf_op jit(solution)/shard_map/ppermute | solution.py:359
  18.8 0.7 %collective-permute-start.5 = (bf16[4,16,8,128]{3,2,1,0:T(8,128)(2,1)S(1)}, bf16[4,16,8,128]{3,2,1,0:T(8,128)(2,1)S(1)}, u32[]{:S(2)}, u32[]{:S(2)}) collective-permute-start(bf16[4,16,8,128]{3,2,1,0:T(8,128)(2,1)S(1)} %constant_dynamic-update-slice_fusion.new.refs_2_), channel_id=1, source_target_pairs={{0,3},{1,4},{2,7},{3,0},{4,1},{5,6},{6,5},{7,2},{8,13},{9,10},{10,... | collective-permute-start | bytes 393224 | tf_op jit(solution)/shard_map/ppermute | solution.py:363
  19.5 0.0 collective-permute-done.2.refs_1_
  19.5 0.4 %collective-permute-start.8 = (bf16[4,16,8,128]{3,2,1,0:T(8,128)(2,1)S(1)}, bf16[4,16,8,128]{3,2,1,0:T(8,128)(2,1)S(1)}, u32[]{:S(2)}, u32[]{:S(2)}) collective-permute-start(bf16[4,16,8,128]{3,2,1,0:T(8,128)(2,1)S(1)} %collective-permute-done.2.refs_1_), channel_id=1, source_target_pairs={{0,1},{1,0},{2,3},{3,2},{4,5},{5,4},{6,7},{7,6},{8,9},{9,8},{10,11... | collective-permute-start | bytes 393224 | tf_op jit(solution)/shard_map/ppermute | solution.py:359
  19.9 1.8 %fetch.1 = (bf16[1152,640]{1,0:T(8,128)(2,1)S(1)}, bf16[1152,640]{1,0:T(8,128)(2,1)S(1)}) custom-call(bf16[1152,640]{1,0:T(8,128)(2,1)} %image_head.3, bf16[1152,640]{1,0:T(8,128)(2,1)} %text_head.3, bf16[4,16,8,128]{3,2,1,0:T(8,128)(2,1)S(1)} %constant_dynamic-update-slice_fusion.new.refs_2_), custom_call_target="tpu_custom_call" | custom-call | flops 67108864 | bytes 2949120 | tf_op jit(solution)/shard_map/fetch/pallas_call | solution.py:389
  21.8 0.0 collective-permute-done.6.refs_4_
  21.8 0.0 collective-permute-done.7.refs_6_
  21.8 1.4 %collective-permute-done.5.refs_3_ = bf16[4,16,8,128]{3,2,1,0:T(8,128)(2,1)S(1)} collective-permute-done((bf16[4,16,8,128]{3,2,1,0:T(8,128)(2,1)S(1)}, bf16[4,16,8,128]{3,2,1,0:T(8,128)(2,1)S(1)}, u32[]{:S(2)}, u32[]{:S(2)}) %collective-permute-start.5) | collective-permute-done | bytes 131104 | tf_op jit(solution)/shard_map/ppermute | solution.py:363
  23.2 0.0 collective-permute-done.8.refs_5_
  23.2 0.1 collective-permute-start.9
  23.2 1.3 %collective-permute-done.9.refs_7_ = bf16[4,16,8,128]{3,2,1,0:T(8,128)(2,1)S(1)} collective-permute-done((bf16[4,16,8,128]{3,2,1,0:T(8,128)(2,1)S(1)}, bf16[4,16,8,128]{3,2,1,0:T(8,128)(2,1)S(1)}, u32[]{:S(2)}, u32[]{:S(2)}) %collective-permute-start.9) | collective-permute-done | bytes 131104 | tf_op jit(solution)/shard_map/ppermute | solution.py:359
  24.5 2.9 %loss.1 = (f32[1]{0:T(128)}, bf16[12,1152]{1,0:T(8,128)(2,1)}, bf16[12,1152]{1,0:T(8,128)(2,1)}, f32[1]{0:T(128)}, f32[1]{0:T(128)}) custom-call(bf16[4,16,8,128]{3,2,1,0:T(8,128)(2,1)S(1)} %pad_maximum_fusion.refs_0_, bf16[4,16,8,128]{3,2,1,0:T(8,128)(2,1)S(1)} %collective-permute-done.2.refs_1_, ...), custom_call_target="tpu_custom_call" | custom-call | tf_op jit(solution)/shard_map/loss/pallas_call | solution.py:414
  (5 shorter events, 0.0 us)
Async XLA Ops:
  3.0 5.5 %collective-permute-start = (bf16[1,16,8,128]{3,2,1,0:T(8,128)(2,1)S(1)}, bf16[1,16,8,128]{3,2,1,0:T(8,128)(2,1)S(1)}, u32[]{:S(2)}, u32[]{:S(2)}) collective-permute-start(bf16[1,16,8,128]{3,2,1,0:T(8,128)(2,1)S(1)} %bitcast.8), channel_id=1, source_target_pairs={{0,17},{1,16},{2,19},{3,18},{4,21},{5,20},{6,23},{7,22},{8,25},{9,... | collective-permute-start | bytes 98312 | tf_op jit(solution)/shard_map/ppermute | solution.py:363
  8.5 3.8 %collective-permute-start.1 = (bf16[2,16,8,128]{3,2,1,0:T(8,128)(2,1)S(1)}, bf16[2,16,8,128]{3,2,1,0:T(8,128)(2,1)S(1)}, u32[]{:S(2)}, u32[]{:S(2)}) collective-permute-start(bf16[2,16,8,128]{3,2,1,0:T(8,128)(2,1)S(1)} %pad_maximum_fusion.1), channel_id=1, source_target_pairs={{0,9},{1,2},{2,1},{3,10},{4,7},{5,12},{6,15},{7,4},{8,11},{9,0},{1... | collective-permute-start | bytes 196616 | tf_op jit(solution)/shard_map/ppermute | solution.py:363
  10.1 3.9 %collective-permute-start.3 = (bf16[2,16,8,128]{3,2,1,0:T(8,128)(2,1)S(1)}, bf16[2,16,8,128]{3,2,1,0:T(8,128)(2,1)S(1)}, u32[]{:S(2)}, u32[]{:S(2)}) collective-permute-start(bf16[2,16,8,128]{3,2,1,0:T(8,128)(2,1)S(1)} %pad_maximum_fusion.1), channel_id=1, source_target_pairs={{0,5},{1,8},{2,11},{3,6},{4,13},{5,0},{6,3},{7,14},{8,1},{9,12},{1... | collective-permute-start | bytes 196616 | tf_op jit(solution)/shard_map/ppermute | solution.py:363
  12.4 9.3 %collective-permute-start.6 = (bf16[4,16,8,128]{3,2,1,0:T(8,128)(2,1)S(1)}, bf16[4,16,8,128]{3,2,1,0:T(8,128)(2,1)S(1)}, u32[]{:S(2)}, u32[]{:S(2)}) collective-permute-start(bf16[4,16,8,128]{3,2,1,0:T(8,128)(2,1)S(1)} %pad_maximum_fusion.refs_0_), channel_id=1, source_target_pairs={{0,1},{1,0},{2,3},{3,2},{4,5},{5,4},{6,7},{7,6},{8,9},{9,8},{10,11... | collective-permute-start | bytes 393224 | tf_op jit(solution)/shard_map/ppermute | solution.py:359
  12.8 6.7 %collective-permute-start.2 = (bf16[4,16,8,128]{3,2,1,0:T(8,128)(2,1)S(1)}, bf16[4,16,8,128]{3,2,1,0:T(8,128)(2,1)S(1)}, u32[]{:S(2)}, u32[]{:S(2)}) collective-permute-start(bf16[4,16,8,128]{3,2,1,0:T(8,128)(2,1)S(1)} %pad_maximum_fusion.refs_0_), channel_id=1, source_target_pairs={{0,3},{1,4},{2,7},{3,0},{4,1},{5,6},{6,5},{7,2},{8,13},{9,10},{10,... | collective-permute-start | bytes 393224 | tf_op jit(solution)/shard_map/ppermute | solution.py:363
  14.0 4.0 %collective-permute-start.4 = (bf16[2,16,8,128]{3,2,1,0:T(8,128)(2,1)S(1)}, bf16[2,16,8,128]{3,2,1,0:T(8,128)(2,1)S(1)}, u32[]{:S(2)}, u32[]{:S(2)}) collective-permute-start(bf16[2,16,8,128]{3,2,1,0:T(8,128)(2,1)S(1)} %collective-permute-done.1), channel_id=1, source_target_pairs={{0,5},{1,8},{2,11},{3,6},{4,13},{5,0},{6,3},{7,14},{8,1},{9,12},{1... | collective-permute-start | bytes 196616 | tf_op jit(solution)/shard_map/ppermute | solution.py:363
  18.0 3.7 %collective-permute-start.7 = (bf16[4,16,8,128]{3,2,1,0:T(8,128)(2,1)S(1)}, bf16[4,16,8,128]{3,2,1,0:T(8,128)(2,1)S(1)}, u32[]{:S(2)}, u32[]{:S(2)}) collective-permute-start(bf16[4,16,8,128]{3,2,1,0:T(8,128)(2,1)S(1)} %constant_dynamic-update-slice_fusion.new.refs_2_), channel_id=1, source_target_pairs={{0,1},{1,0},{2,3},{3,2},{4,5},{5,4},{6,7},{7,6},{8,9},{9,8},{10,11... | collective-permute-start | bytes 393224 | tf_op jit(solution)/shard_map/ppermute | solution.py:359
  18.8 4.4 %collective-permute-start.5 = (bf16[4,16,8,128]{3,2,1,0:T(8,128)(2,1)S(1)}, bf16[4,16,8,128]{3,2,1,0:T(8,128)(2,1)S(1)}, u32[]{:S(2)}, u32[]{:S(2)}) collective-permute-start(bf16[4,16,8,128]{3,2,1,0:T(8,128)(2,1)S(1)} %constant_dynamic-update-slice_fusion.new.refs_2_), channel_id=1, source_target_pairs={{0,3},{1,4},{2,7},{3,0},{4,1},{5,6},{6,5},{7,2},{8,13},{9,10},{10,... | collective-permute-start | bytes 393224 | tf_op jit(solution)/shard_map/ppermute | solution.py:363
  19.5 3.7 %collective-permute-start.8 = (bf16[4,16,8,128]{3,2,1,0:T(8,128)(2,1)S(1)}, bf16[4,16,8,128]{3,2,1,0:T(8,128)(2,1)S(1)}, u32[]{:S(2)}, u32[]{:S(2)}) collective-permute-start(bf16[4,16,8,128]{3,2,1,0:T(8,128)(2,1)S(1)} %collective-permute-done.2.refs_1_), channel_id=1, source_target_pairs={{0,1},{1,0},{2,3},{3,2},{4,5},{5,4},{6,7},{7,6},{8,9},{9,8},{10,11... | collective-permute-start | bytes 393224 | tf_op jit(solution)/shard_map/ppermute | solution.py:359
  23.2 1.3 %collective-permute-start.9 = (bf16[4,16,8,128]{3,2,1,0:T(8,128)(2,1)S(1)}, bf16[4,16,8,128]{3,2,1,0:T(8,128)(2,1)S(1)}, u32[]{:S(2)}, u32[]{:S(2)}) collective-permute-start(bf16[4,16,8,128]{3,2,1,0:T(8,128)(2,1)S(1)} %collective-permute-done.5.refs_3_), channel_id=1, source_target_pairs={{0,1},{1,0},{2,3},{3,2},{4,5},{5,4},{6,7},{7,6},{8,9},{9,8},{10,11... | collective-permute-start | bytes 393224 | tf_op jit(solution)/shard_map/ppermute | solution.py:359

commit v2 on v1

--- a/solution.py
+++ b/solution.py
@@ -14,6 +14,7 @@
 BITS = 32
 LOGIT_BUDGET = 4 << 20
 SIDE_FLOPS = 1 << 26
+HOPS = 4
 
 
 def normalize(projected):
@@ -152,7 +153,8 @@
 def hop_orders(devices):
     bits = [1 << level for level in reversed(range(1, devices.bit_length() - 1))]
     first, rest = bits[:1], bits[1:]
-    return first + rest, first + [rest[2], rest[0], rest[1]]
+    rest = rest[-1:] + rest[:-1]
+    return first + rest, first + rest[::-1]
 
 
 def parity(number, bits):
@@ -444,8 +446,7 @@
     pairs = image_feats.shape[0] * devices
     small = (
         4 * pairs * pairs <= LOGIT_BUDGET
-        and devices >= 8
-        and devices & (devices - 1) == 0
+        and devices == 2 << HOPS
         and image_head.shape[1] % LANES == 0
         and 2 * image_feats.shape[0] % TILE == 0
         and 2 * image_feats.shape[0] // TILE * BITS <= LANES

time: 27.6 us -> 27.6 us (level)
  the two profiles are of different devices: /device:TPU:25 before, /device:TPU:0 now
where the time goes in v2:
time: 27.6 us; the launch traced here: 27.4 us
  starting transfers between devices  12.5 us (45%)
  Pallas kernels  7.14 us (26%)
  waiting for transfers between devices  5.72 us (21%)
  between operations  1.99 us (7%)
    ppermute x6, starting transfers between devices, hop(): return lax.ppermute(array, 'dev', pairs)  11 us
    ppermute x6, waiting for transfers between devices, hop(): return lax.ppermute(array, 'dev', pairs)  4.72 us
    pallas_call x1, Pallas kernels, on_device_small(): pl.pallas_call(functools.partial(loss_kernel, chips, rows * devices, orde...  2.92 us
    pallas_call x1, Pallas kernels, on_device_small(): pl.pallas_call(project_kernel, out_shape=(jax.ShapeDtypeStruct((tiles, TI...  2.38 us
    pallas_call x1, Pallas kernels, on_device_small(): pl.pallas_call(fetch_kernel, out_shape=(jax.ShapeDtypeStruct((depth, widt...  1.83 us
    ppermute x4, starting transfers between devices, swap(): return lax.ppermute(array, 'dev', [(i, i ^ 1) for i in range(devices)])  1.54 us
    ppermute x4, waiting for transfers between devices, swap(): return lax.ppermute(array, 'dev', [(i, i ^ 1) for i in range(devices)])  0.99 us
  transfers between devices with their start and end apart: 10, of which 5 were waited for; matrix products, arithmetic and copies ran while one was open for 0% of the time, Pallas kernels for 7%

profile of v2, /device:TPU:0, one launch (start us, length us, event | category | flops | bytes accessed | tf_op | source)
XLA Modules:
  0.0 27.4 jit_solution(12077251039279148416)
XLA Ops:
  0.6 2.4 %project.1 = (bf16[16,8,128]{2,1,0:T(8,128)(2,1)S(1)}, f32[12,768]{1,0:T(8,128)S(1)}, f32[12,768]{1,0:T(8,128)S(1)}) custom-call(s32[12]{0:T(128)} %image_ids.1, s32[12]{0:T(128)} %text_ids.1, bf16[12,1152]{1,0:T(8,128)(2,1)} %image_feats.1, bf16[12,1152]{1,0:T(8,128)(2,1)} %text_feats.1, bf16[1152,640]{1,0:T(8,128)(2,1)} %image_head.3, ...), custom_call_target="tpu_custom_call" | custom-call | tf_op jit(solution)/shard_map/project/pallas_call | solution.py:328
  3.0 3.6 %collective-permute-start = (bf16[1,16,8,128]{3,2,1,0:T(8,128)(2,1)S(1)}, bf16[1,16,8,128]{3,2,1,0:T(8,128)(2,1)S(1)}, u32[]{:S(2)}, u32[]{:S(2)}) collective-permute-start(bf16[1,16,8,128]{3,2,1,0:T(8,128)(2,1)S(1)} %bitcast.8), channel_id=1, source_target_pairs={{0,17},{1,16},{2,19},{3,18},{4,21},{5,20},{6,23},{7,22},{8,25},{9,... | collective-permute-start | bytes 98312 | tf_op jit(solution)/shard_map/ppermute | solution.py:365
  7.9 0.5 %collective-permute-done = bf16[1,16,8,128]{3,2,1,0:T(8,128)(2,1)S(1)} collective-permute-done((bf16[1,16,8,128]{3,2,1,0:T(8,128)(2,1)S(1)}, bf16[1,16,8,128]{3,2,1,0:T(8,128)(2,1)S(1)}, u32[]{:S(2)}, u32[]{:S(2)}) %collective-permute-start) | collective-permute-done | bytes 32800 | tf_op jit(solution)/shard_map/ppermute | solution.py:365
  8.4 1.8 %collective-permute-start.1 = (bf16[2,16,8,128]{3,2,1,0:T(8,128)(2,1)S(1)}, bf16[2,16,8,128]{3,2,1,0:T(8,128)(2,1)S(1)}, u32[]{:S(2)}, u32[]{:S(2)}) collective-permute-start(bf16[2,16,8,128]{3,2,1,0:T(8,128)(2,1)S(1)} %pad_maximum_fusion.1), channel_id=1, source_target_pairs={{0,3},{1,4},{2,7},{3,0},{4,1},{5,6},{6,5},{7,2},{8,13},{9,10},{10,... | collective-permute-start | bytes 196616 | tf_op jit(solution)/shard_map/ppermute | solution.py:365
  10.2 1.6 %collective-permute-start.3 = (bf16[2,16,8,128]{3,2,1,0:T(8,128)(2,1)S(1)}, bf16[2,16,8,128]{3,2,1,0:T(8,128)(2,1)S(1)}, u32[]{:S(2)}, u32[]{:S(2)}) collective-permute-start(bf16[2,16,8,128]{3,2,1,0:T(8,128)(2,1)S(1)} %pad_maximum_fusion.1), channel_id=1, source_target_pairs={{0,9},{1,8},{2,11},{3,10},{4,13},{5,12},{6,15},{7,14},{8,1},{9,0},... | collective-permute-start | bytes 196616 | tf_op jit(solution)/shard_map/ppermute | solution.py:365
  11.8 0.4 %collective-permute-done.1 = bf16[2,16,8,128]{3,2,1,0:T(8,128)(2,1)S(1)} collective-permute-done((bf16[2,16,8,128]{3,2,1,0:T(8,128)(2,1)S(1)}, bf16[2,16,8,128]{3,2,1,0:T(8,128)(2,1)S(1)}, u32[]{:S(2)}, u32[]{:S(2)}) %collective-permute-start.1) | collective-permute-done | bytes 65568 | tf_op jit(solution)/shard_map/ppermute | solution.py:365
  12.2 0.6 %collective-permute-start.6 = (bf16[4,16,8,128]{3,2,1,0:T(8,128)(2,1)S(1)}, bf16[4,16,8,128]{3,2,1,0:T(8,128)(2,1)S(1)}, u32[]{:S(2)}, u32[]{:S(2)}) collective-permute-start(bf16[4,16,8,128]{3,2,1,0:T(8,128)(2,1)S(1)} %pad_maximum_fusion.refs_0_), channel_id=1, source_target_pairs={{0,1},{1,0},{2,3},{3,2},{4,5},{5,4},{6,7},{7,6},{8,9},{9,8},{10,11... | collective-permute-start | bytes 393224 | tf_op jit(solution)/shard_map/ppermute | solution.py:361
  12.7 1.7 %collective-permute-start.2 = (bf16[4,16,8,128]{3,2,1,0:T(8,128)(2,1)S(1)}, bf16[4,16,8,128]{3,2,1,0:T(8,128)(2,1)S(1)}, u32[]{:S(2)}, u32[]{:S(2)}) collective-permute-start(bf16[4,16,8,128]{3,2,1,0:T(8,128)(2,1)S(1)} %pad_maximum_fusion.refs_0_), channel_id=1, source_target_pairs={{0,5},{1,2},{2,1},{3,6},{4,7},{5,0},{6,3},{7,4},{8,11},{9,12},{10,... | collective-permute-start | bytes 393224 | tf_op jit(solution)/shard_map/ppermute | solution.py:365
  14.4 1.3 %collective-permute-start.4 = (bf16[2,16,8,128]{3,2,1,0:T(8,128)(2,1)S(1)}, bf16[2,16,8,128]{3,2,1,0:T(8,128)(2,1)S(1)}, u32[]{:S(2)}, u32[]{:S(2)}) collective-permute-start(bf16[2,16,8,128]{3,2,1,0:T(8,128)(2,1)S(1)} %collective-permute-done.1), channel_id=1, source_target_pairs={{0,9},{1,8},{2,11},{3,10},{4,13},{5,12},{6,15},{7,14},{8,1},{9,0},... | collective-permute-start | bytes 196616 | tf_op jit(solution)/shard_map/ppermute | solution.py:365
  15.7 0.0 collective-permute-done.3
  15.7 2.8 %collective-permute-done.4 = bf16[2,16,8,128]{3,2,1,0:T(8,128)(2,1)S(1)} collective-permute-done((bf16[2,16,8,128]{3,2,1,0:T(8,128)(2,1)S(1)}, bf16[2,16,8,128]{3,2,1,0:T(8,128)(2,1)S(1)}, u32[]{:S(2)}, u32[]{:S(2)}) %collective-permute-start.4) | collective-permute-done | bytes 65568 | tf_op jit(solution)/shard_map/ppermute | solution.py:365
  18.5 0.2 collective-permute-start.7
  18.7 1.1 %collective-permute-start.5 = (bf16[4,16,8,128]{3,2,1,0:T(8,128)(2,1)S(1)}, bf16[4,16,8,128]{3,2,1,0:T(8,128)(2,1)S(1)}, u32[]{:S(2)}, u32[]{:S(2)}) collective-permute-start(bf16[4,16,8,128]{3,2,1,0:T(8,128)(2,1)S(1)} %constant_dynamic-update-slice_fusion.new.refs_2_), channel_id=1, source_target_pairs={{0,5},{1,2},{2,1},{3,6},{4,7},{5,0},{6,3},{7,4},{8,11},{9,12},{10,... | collective-permute-start | bytes 393224 | tf_op jit(solution)/shard_map/ppermute | solution.py:365
  19.8 0.0 collective-permute-done.2.refs_1_
  19.8 0.4 %collective-permute-start.8 = (bf16[4,16,8,128]{3,2,1,0:T(8,128)(2,1)S(1)}, bf16[4,16,8,128]{3,2,1,0:T(8,128)(2,1)S(1)}, u32[]{:S(2)}, u32[]{:S(2)}) collective-permute-start(bf16[4,16,8,128]{3,2,1,0:T(8,128)(2,1)S(1)} %collective-permute-done.2.refs_1_), channel_id=1, source_target_pairs={{0,1},{1,0},{2,3},{3,2},{4,5},{5,4},{6,7},{7,6},{8,9},{9,8},{10,11... | collective-permute-start | bytes 393224 | tf_op jit(solution)/shard_map/ppermute | solution.py:361
  20.2 1.8 %fetch.1 = (bf16[1152,640]{1,0:T(8,128)(2,1)S(1)}, bf16[1152,640]{1,0:T(8,128)(2,1)S(1)}) custom-call(bf16[1152,640]{1,0:T(8,128)(2,1)} %image_head.3, bf16[1152,640]{1,0:T(8,128)(2,1)} %text_head.3, bf16[4,16,8,128]{3,2,1,0:T(8,128)(2,1)S(1)} %constant_dynamic-update-slice_fusion.new.refs_2_), custom_call_target="tpu_custom_call" | custom-call | flops 67108864 | bytes 2949120 | tf_op jit(solution)/shard_map/fetch/pallas_call | solution.py:391
  22.0 0.0 collective-permute-done.6.refs_4_
  22.0 0.0 collective-permute-done.7.refs_6_
  22.0 1.1 %collective-permute-done.5.refs_3_ = bf16[4,16,8,128]{3,2,1,0:T(8,128)(2,1)S(1)} collective-permute-done((bf16[4,16,8,128]{3,2,1,0:T(8,128)(2,1)S(1)}, bf16[4,16,8,128]{3,2,1,0:T(8,128)(2,1)S(1)}, u32[]{:S(2)}, u32[]{:S(2)}) %collective-permute-start.5) | collective-permute-done | bytes 131104 | tf_op jit(solution)/shard_map/ppermute | solution.py:365
  23.1 0.0 collective-permute-done.8.refs_5_
  23.1 0.4 %collective-permute-start.9 = (bf16[4,16,8,128]{3,2,1,0:T(8,128)(2,1)S(1)}, bf16[4,16,8,128]{3,2,1,0:T(8,128)(2,1)S(1)}, u32[]{:S(2)}, u32[]{:S(2)}) collective-permute-start(bf16[4,16,8,128]{3,2,1,0:T(8,128)(2,1)S(1)} %collective-permute-done.5.refs_3_), channel_id=1, source_target_pairs={{0,1},{1,0},{2,3},{3,2},{4,5},{5,4},{6,7},{7,6},{8,9},{9,8},{10,11... | collective-permute-start | bytes 393224 | tf_op jit(solution)/shard_map/ppermute | solution.py:361
  23.5 1.0 %collective-permute-done.9.refs_7_ = bf16[4,16,8,128]{3,2,1,0:T(8,128)(2,1)S(1)} collective-permute-done((bf16[4,16,8,128]{3,2,1,0:T(8,128)(2,1)S(1)}, bf16[4,16,8,128]{3,2,1,0:T(8,128)(2,1)S(1)}, u32[]{:S(2)}, u32[]{:S(2)}) %collective-permute-start.9) | collective-permute-done | bytes 131104 | tf_op jit(solution)/shard_map/ppermute | solution.py:361
  24.5 2.9 %loss.1 = (f32[1]{0:T(128)}, bf16[12,1152]{1,0:T(8,128)(2,1)}, bf16[12,1152]{1,0:T(8,128)(2,1)}, f32[1]{0:T(128)}, f32[1]{0:T(128)}) custom-call(bf16[4,16,8,128]{3,2,1,0:T(8,128)(2,1)S(1)} %pad_maximum_fusion.refs_0_, bf16[4,16,8,128]{3,2,1,0:T(8,128)(2,1)S(1)} %collective-permute-done.2.refs_1_, ...), custom_call_target="tpu_custom_call" | custom-call | tf_op jit(solution)/shard_map/loss/pallas_call | solution.py:416
  (5 shorter events, 0.0 us)
Async XLA Ops:
  3.0 5.4 %collective-permute-start = (bf16[1,16,8,128]{3,2,1,0:T(8,128)(2,1)S(1)}, bf16[1,16,8,128]{3,2,1,0:T(8,128)(2,1)S(1)}, u32[]{:S(2)}, u32[]{:S(2)}) collective-permute-start(bf16[1,16,8,128]{3,2,1,0:T(8,128)(2,1)S(1)} %bitcast.8), channel_id=1, source_target_pairs={{0,17},{1,16},{2,19},{3,18},{4,21},{5,20},{6,23},{7,22},{8,25},{9,... | collective-permute-start | bytes 98312 | tf_op jit(solution)/shard_map/ppermute | solution.py:365
  8.4 3.8 %collective-permute-start.1 = (bf16[2,16,8,128]{3,2,1,0:T(8,128)(2,1)S(1)}, bf16[2,16,8,128]{3,2,1,0:T(8,128)(2,1)S(1)}, u32[]{:S(2)}, u32[]{:S(2)}) collective-permute-start(bf16[2,16,8,128]{3,2,1,0:T(8,128)(2,1)S(1)} %pad_maximum_fusion.1), channel_id=1, source_target_pairs={{0,3},{1,4},{2,7},{3,0},{4,1},{5,6},{6,5},{7,2},{8,13},{9,10},{10,... | collective-permute-start | bytes 196616 | tf_op jit(solution)/shard_map/ppermute | solution.py:365
  10.2 5.5 %collective-permute-start.3 = (bf16[2,16,8,128]{3,2,1,0:T(8,128)(2,1)S(1)}, bf16[2,16,8,128]{3,2,1,0:T(8,128)(2,1)S(1)}, u32[]{:S(2)}, u32[]{:S(2)}) collective-permute-start(bf16[2,16,8,128]{3,2,1,0:T(8,128)(2,1)S(1)} %pad_maximum_fusion.1), channel_id=1, source_target_pairs={{0,9},{1,8},{2,11},{3,10},{4,13},{5,12},{6,15},{7,14},{8,1},{9,0},... | collective-permute-start | bytes 196616 | tf_op jit(solution)/shard_map/ppermute | solution.py:365
  12.2 9.9 %collective-permute-start.6 = (bf16[4,16,8,128]{3,2,1,0:T(8,128)(2,1)S(1)}, bf16[4,16,8,128]{3,2,1,0:T(8,128)(2,1)S(1)}, u32[]{:S(2)}, u32[]{:S(2)}) collective-permute-start(bf16[4,16,8,128]{3,2,1,0:T(8,128)(2,1)S(1)} %pad_maximum_fusion.refs_0_), channel_id=1, source_target_pairs={{0,1},{1,0},{2,3},{3,2},{4,5},{5,4},{6,7},{7,6},{8,9},{9,8},{10,11... | collective-permute-start | bytes 393224 | tf_op jit(solution)/shard_map/ppermute | solution.py:361
  12.7 7.1 %collective-permute-start.2 = (bf16[4,16,8,128]{3,2,1,0:T(8,128)(2,1)S(1)}, bf16[4,16,8,128]{3,2,1,0:T(8,128)(2,1)S(1)}, u32[]{:S(2)}, u32[]{:S(2)}) collective-permute-start(bf16[4,16,8,128]{3,2,1,0:T(8,128)(2,1)S(1)} %pad_maximum_fusion.refs_0_), channel_id=1, source_target_pairs={{0,5},{1,2},{2,1},{3,6},{4,7},{5,0},{6,3},{7,4},{8,11},{9,12},{10,... | collective-permute-start | bytes 393224 | tf_op jit(solution)/shard_map/ppermute | solution.py:365
  14.4 4.1 %collective-permute-start.4 = (bf16[2,16,8,128]{3,2,1,0:T(8,128)(2,1)S(1)}, bf16[2,16,8,128]{3,2,1,0:T(8,128)(2,1)S(1)}, u32[]{:S(2)}, u32[]{:S(2)}) collective-permute-start(bf16[2,16,8,128]{3,2,1,0:T(8,128)(2,1)S(1)} %collective-permute-done.1), channel_id=1, source_target_pairs={{0,9},{1,8},{2,11},{3,10},{4,13},{5,12},{6,15},{7,14},{8,1},{9,0},... | collective-permute-start | bytes 196616 | tf_op jit(solution)/shard_map/ppermute | solution.py:365
  18.5 3.5 %collective-permute-start.7 = (bf16[4,16,8,128]{3,2,1,0:T(8,128)(2,1)S(1)}, bf16[4,16,8,128]{3,2,1,0:T(8,128)(2,1)S(1)}, u32[]{:S(2)}, u32[]{:S(2)}) collective-permute-start(bf16[4,16,8,128]{3,2,1,0:T(8,128)(2,1)S(1)} %constant_dynamic-update-slice_fusion.new.refs_2_), channel_id=1, source_target_pairs={{0,1},{1,0},{2,3},{3,2},{4,5},{5,4},{6,7},{7,6},{8,9},{9,8},{10,11... | collective-permute-start | bytes 393224 | tf_op jit(solution)/shard_map/ppermute | solution.py:361
  18.7 4.4 %collective-permute-start.5 = (bf16[4,16,8,128]{3,2,1,0:T(8,128)(2,1)S(1)}, bf16[4,16,8,128]{3,2,1,0:T(8,128)(2,1)S(1)}, u32[]{:S(2)}, u32[]{:S(2)}) collective-permute-start(bf16[4,16,8,128]{3,2,1,0:T(8,128)(2,1)S(1)} %constant_dynamic-update-slice_fusion.new.refs_2_), channel_id=1, source_target_pairs={{0,5},{1,2},{2,1},{3,6},{4,7},{5,0},{6,3},{7,4},{8,11},{9,12},{10,... | collective-permute-start | bytes 393224 | tf_op jit(solution)/shard_map/ppermute | solution.py:365
  19.8 3.3 %collective-permute-start.8 = (bf16[4,16,8,128]{3,2,1,0:T(8,128)(2,1)S(1)}, bf16[4,16,8,128]{3,2,1,0:T(8,128)(2,1)S(1)}, u32[]{:S(2)}, u32[]{:S(2)}) collective-permute-start(bf16[4,16,8,128]{3,2,1,0:T(8,128)(2,1)S(1)} %collective-permute-done.2.refs_1_), channel_id=1, source_target_pairs={{0,1},{1,0},{2,3},{3,2},{4,5},{5,4},{6,7},{7,6},{8,9},{9,8},{10,11... | collective-permute-start | bytes 393224 | tf_op jit(solution)/shard_map/ppermute | solution.py:361
  23.1 1.4 %collective-permute-start.9 = (bf16[4,16,8,128]{3,2,1,0:T(8,128)(2,1)S(1)}, bf16[4,16,8,128]{3,2,1,0:T(8,128)(2,1)S(1)}, u32[]{:S(2)}, u32[]{:S(2)}) collective-permute-start(bf16[4,16,8,128]{3,2,1,0:T(8,128)(2,1)S(1)} %collective-permute-done.5.refs_3_), channel_id=1, source_target_pairs={{0,1},{1,0},{2,3},{3,2},{4,5},{5,4},{6,7},{7,6},{8,9},{9,8},{10,11... | collective-permute-start | bytes 393224 | tf_op jit(solution)/shard_map/ppermute | solution.py:361
